TPU v7x, 32 devices: a whole 2x2x4 slice. The times are simulated.
32 devices in a mesh: grp: 8 (over z, x), sp: 4 (over y, core).
Axes of the slice: x: 2, y: 2, z: 4, core: 2. Of those that a mesh axis runs over, the one named last changes fastest.
Arguments:
- query_rows: bfloat16 [4096, 4096], P(('grp', 'sp')), parts along dimension 0, may hold values from -250 to 250
- key_rows: bfloat16 [4096, 1024], P(('grp', 'sp')), parts along dimension 0, may hold values from -4 to 4
- value_rows: bfloat16 [4096, 1024], P(('grp', 'sp')), parts along dimension 0, may hold values from -6 to 6
- out_grad: bfloat16 [4096, 4096], P(('grp', 'sp')), parts along dimension 0, may hold values from -6 to 6
- question_lengths: int32 [64], P('grp'), parts along dimension 0, may hold values from 1 to 128, 256 in all
Outputs:
- query_grad: bfloat16 [4096, 4096], P(('grp', 'sp')), parts along dimension 0
- key_grad: bfloat16 [4096, 1024], P(('grp', 'sp')), parts along dimension 0
- value_grad: bfloat16 [4096, 1024], P(('grp', 'sp')), parts along dimension 0
There are 8 independent parts, one for each index of `grp`. A program takes and returns all parts, laid end to end along the dimension named above; each array names one. Nothing has to cross between parts.
All inputs are finite; a program needn't handle non-finite values.
Results may differ from a plain program's by a relative error of at most 0.033.
Values may be sent and summed in bfloat16 or wider, within the bound.
No kernel may reach another device: no remote copies, remote signals or barrier semaphores. Data moves between devices by JAX's collectives and lax.ppermute only.
A program may use at most 128 MiB of HBM per device.

v0:
```python
from functools import partial
from functools import reduce
import math
import jax
import jax.numpy as jnp
from jax import lax
from jax.sharding import PartitionSpec as P

HD = 128
QH = 32
KVH = 8
MASKED = -1e30


def widen(rows, copies):
    tokens = rows.shape[0]
    shaped = rows.reshape(tokens, KVH, 1, HD)
    return jnp.broadcast_to(shaped, (tokens, KVH, copies, HD)).reshape(tokens, KVH * copies * HD)


def segment_ids(question_lengths, length, doc_len):
    ends = jnp.cumsum(question_lengths)
    places = jnp.arange(length, dtype=jnp.int32)
    inside = jnp.sum((ends[None, :] <= (places - doc_len)[:, None]).astype(jnp.int32), axis=1)
    return jnp.where(places < doc_len, -1, inside)


def make_scores(query_block, key_block, visible, scaling):
    raw = (
        jnp.einsum("bkgd,skd->kgbs", query_block, key_block, preferred_element_type=jnp.float32)
        * scaling
    )
    return jnp.where(visible[None, None], raw, MASKED)


def weighted_values(probs_b, value_block):
    return jnp.einsum("kgbs,skd->bkgd", probs_b, value_block, preferred_element_type=jnp.float32)


def backward_block(probs, probs_b, delta, grad_block, query_block, key_block, value_block, scaling):
    value_part = jnp.einsum(
        "kgbs,bkgd->skd", probs_b, grad_block, preferred_element_type=jnp.float32
    )
    prob_grad = jnp.einsum(
        "bkgd,skd->kgbs", grad_block, value_block, preferred_element_type=jnp.float32
    )
    score_grad = (probs * (prob_grad - delta[..., None])).astype(jnp.bfloat16)
    query_part = jnp.einsum(
        "kgbs,skd->bkgd", score_grad, key_block, preferred_element_type=jnp.float32
    )
    key_part = (
        jnp.einsum("kgbs,bkgd->skd", score_grad, query_block, preferred_element_type=jnp.float32)
        * scaling
    )
    return (query_part, key_part, value_part)


def on_device(query_rows, key_rows, value_rows, out_grad, question_lengths):
    devices = lax.axis_size("sp")
    tokens = query_rows.shape[0]
    length = tokens * devices
    doc_len = length // 2
    block_len = min(512, length)
    block_count = length // block_len
    scaling = 1.0 / math.sqrt(HD)
    copies = max(KVH, devices) // KVH
    keys_local, values_local = (
        lax.all_to_all(widen(key_rows, copies), "sp", split_axis=1, concat_axis=0, tiled=True),
        lax.all_to_all(widen(value_rows, copies), "sp", split_axis=1, concat_axis=0, tiled=True),
    )
    queries_local, grads_local = (
        lax.all_to_all(query_rows, "sp", split_axis=1, concat_axis=0, tiled=True),
        lax.all_to_all(out_grad, "sp", split_axis=1, concat_axis=0, tiled=True),
    )
    key_heads = KVH * copies // devices
    per_group = QH // devices // key_heads
    queries = queries_local.reshape(length, key_heads, per_group, HD)
    grads = grads_local.reshape(length, key_heads, per_group, HD)
    keys = keys_local.reshape(length, key_heads, HD)
    values = values_local.reshape(length, key_heads, HD)
    segment = segment_ids(question_lengths, length, doc_len)
    places = jnp.arange(length, dtype=jnp.int32)
    query_shape = (block_len, key_heads, per_group, HD)
    key_shape = (block_len, key_heads, HD)
    key_sums = [jnp.zeros(key_shape, jnp.float32)] * block_count
    value_sums = [jnp.zeros(key_shape, jnp.float32)] * block_count
    query_parts = []
    for row_block in range(block_count):
        row_start = row_block * block_len
        query_block = queries[row_start : row_start + block_len]
        grad_block = grads[row_start : row_start + block_len]
        row_places = places[row_start : row_start + block_len]
        row_segment = segment[row_start : row_start + block_len]
        needs = []
        scores = []
        for col_block in range(row_block + 1):
            col_start = col_block * block_len
            col_places = places[col_start : col_start + block_len]
            col_segment = segment[col_start : col_start + block_len]
            visible = (col_places[None, :] <= row_places[:, None]) & (
                (col_places[None, :] < doc_len) | (col_segment[None, :] == row_segment[:, None])
            )
            needed = True
            needs.append(needed)
            scores.append(
                make_scores(query_block, keys[col_start : col_start + block_len], visible, scaling)
            )
        peak = reduce(jnp.maximum, [jnp.max(score, axis=3) for score in scores])
        total = reduce(
            jnp.add, [jnp.sum(jnp.exp(score - peak[..., None]), axis=3) for score in scores]
        )
        log_total = peak + jnp.log(total)
        probs = [jnp.exp(score - log_total[..., None]) for score in scores]
        probs_low = [single.astype(jnp.bfloat16) for single in probs]
        output = jnp.zeros(query_shape, jnp.float32)
        for col_block in range(row_block + 1):
            col_start = col_block * block_len
            output = output + weighted_values(
                probs_low[col_block], values[col_start : col_start + block_len]
            )
        output_low = output.astype(jnp.bfloat16)
        delta = jnp.einsum(
            "bkgd,bkgd->kgb", grad_block, output_low, preferred_element_type=jnp.float32
        )
        query_sum = jnp.zeros(query_shape, jnp.float32)
        for col_block in range(row_block + 1):
            col_start = col_block * block_len
            action = partial(
                backward_block,
                probs[col_block],
                probs_low[col_block],
                delta,
                grad_block,
                query_block,
                keys[col_start : col_start + block_len],
                values[col_start : col_start + block_len],
                scaling,
            )
            query_part, key_part, value_part = action()
            query_sum = query_sum + query_part
            key_sums[col_block] = key_sums[col_block] + key_part
            value_sums[col_block] = value_sums[col_block] + value_part
        query_parts.append((query_sum * scaling).astype(jnp.bfloat16))
    query_local = jnp.concatenate(query_parts, axis=0).reshape(length, key_heads * per_group * HD)
    key_local = jnp.concatenate(key_sums, axis=0).reshape(length, key_heads * HD)
    value_local = jnp.concatenate(value_sums, axis=0).reshape(length, key_heads * HD)
    query_grad = lax.all_to_all(query_local, "sp", split_axis=0, concat_axis=1, tiled=True)
    key_back, value_back = (
        lax.all_to_all(key_local, "sp", split_axis=0, concat_axis=1, tiled=True),
        lax.all_to_all(value_local, "sp", split_axis=0, concat_axis=1, tiled=True),
    )
    key_grad = (
        jnp.sum(key_back.reshape(tokens, KVH, copies, HD), axis=2)
        .reshape(tokens, KVH * HD)
        .astype(jnp.bfloat16)
    )
    value_grad = (
        jnp.sum(value_back.reshape(tokens, KVH, copies, HD), axis=2)
        .reshape(tokens, KVH * HD)
        .astype(jnp.bfloat16)
    )
    return (query_grad, key_grad, value_grad)


def solution(mesh):
    return jax.shard_map(
        on_device,
        mesh=mesh,
        in_specs=(
            P(("grp", "sp"), None),
            P(("grp", "sp"), None),
            P(("grp", "sp"), None),
            P(("grp", "sp"), None),
            P("grp"),
        ),
        out_specs=(P(("grp", "sp"), None), P(("grp", "sp"), None), P(("grp", "sp"), None)),
        check_vma=False,
    )
```

profile of v0, /device:TPU:0, one launch (start us, length us, event | category | flops | bytes accessed | tf_op | source)
XLA Modules:
  0.0 117.2 jit_solution(11566615232329075632)
XLA Ops:
  0.6 1.7 %copy.125 = bf16[16,4,8,256]{3,2,0,1:T(8,128)(2,1)} copy(bf16[16,4,8,256]{3,2,1,0:T(8,128)(2,1)} %bitcast.94) | data formatting | bytes 524288 | tf_op jit(solution)/shard_map/all_to_all | solution.py:68
  2.3 4.3 %all-to-all-start = ((bf16[128,4,256]{2,0,1:T(8,128)(2,1)}), bf16[128,4,256]{2,0,1:T(8,128)(2,1)S(1)}, u32[]{:S(2)}, u32[]{:S(2)}) async-start(bf16[128,4,256]{2,0,1:T(8,128)(2,1)} %bitcast.76), calls=%async_computation | async-start | bytes 524288 | tf_op jit(solution)/shard_map/all_to_all | solution.py:68
  6.6 1.7 %copy.124 = bf16[16,4,8,256]{3,2,0,1:T(8,128)(2,1)} copy(bf16[16,4,8,256]{3,2,1,0:T(8,128)(2,1)} %bitcast.95) | data formatting | bytes 524288 | tf_op jit(solution)/shard_map/all_to_all | solution.py:69
  8.2 4.3 %all-to-all-done = bf16[128,4,256]{2,0,1:T(8,128)(2,1)S(1)} async-done(((bf16[128,4,256]{2,0,1:T(8,128)(2,1)}), bf16[128,4,256]{2,0,1:T(8,128)(2,1)S(1)}, u32[]{:S(2)}, u32[]{:S(2)}) %all-to-all-start) | async-done | bytes 262176 | tf_op jit(solution)/shard_map/all_to_all | solution.py:68
  12.6 3.4 %all-to-all-start.2 = ((bf16[128,4,256]{2,0,1:T(8,128)(2,1)}), bf16[128,4,256]{2,0,1:T(8,128)(2,1)S(1)}, u32[]{:S(2)}, u32[]{:S(2)}) async-start(bf16[128,4,256]{2,0,1:T(8,128)(2,1)} %bitcast.75), calls=%async_computation.2 | async-start | bytes 524288 | tf_op jit(solution)/shard_map/all_to_all | solution.py:69
  16.0 2.3 %copy.123 = bf16[16,4,8,1024]{3,2,0,1:T(8,128)(2,1)} copy(bf16[16,4,8,1024]{3,2,1,0:T(8,128)(2,1)} %bitcast.84) | data formatting | bytes 2097152 | tf_op jit(solution)/shard_map/all_to_all | solution.py:72
  18.3 3.7 %all-to-all-done.2 = bf16[128,4,256]{2,0,1:T(8,128)(2,1)S(1)} async-done(((bf16[128,4,256]{2,0,1:T(8,128)(2,1)}), bf16[128,4,256]{2,0,1:T(8,128)(2,1)S(1)}, u32[]{:S(2)}, u32[]{:S(2)}) %all-to-all-start.2) | async-done | bytes 262176 | tf_op jit(solution)/shard_map/all_to_all | solution.py:69
  22.0 3.5 %all-to-all-start.1 = ((bf16[128,4,1024]{2,0,1:T(8,128)(2,1)}), bf16[128,4,1024]{2,0,1:T(8,128)(2,1)S(1)}, u32[]{:S(2)}, u32[]{:S(2)}) async-start(bf16[128,4,1024]{2,0,1:T(8,128)(2,1)} %bitcast.74), calls=%async_computation.1 | async-start | bytes 2097152 | tf_op jit(solution)/shard_map/all_to_all | solution.py:72
  25.5 2.3 %copy.122 = bf16[16,4,8,1024]{3,2,0,1:T(8,128)(2,1)} copy(bf16[16,4,8,1024]{3,2,1,0:T(8,128)(2,1)} %bitcast.85) | data formatting | bytes 2097152 | tf_op jit(solution)/shard_map/all_to_all | solution.py:73
  28.0 11.9 %all-to-all-done.1 = bf16[128,4,1024]{2,0,1:T(8,128)(2,1)S(1)} async-done(((bf16[128,4,1024]{2,0,1:T(8,128)(2,1)}), bf16[128,4,1024]{2,0,1:T(8,128)(2,1)S(1)}, u32[]{:S(2)}, u32[]{:S(2)}) %all-to-all-start.1) | async-done | bytes 1048608 | tf_op jit(solution)/shard_map/all_to_all | solution.py:72
  39.9 3.5 %all-to-all-start.3 = ((bf16[128,4,1024]{2,0,1:T(8,128)(2,1)}), bf16[128,4,1024]{2,0,1:T(8,128)(2,1)S(1)}, u32[]{:S(2)}, u32[]{:S(2)}) async-start(bf16[128,4,1024]{2,0,1:T(8,128)(2,1)} %bitcast.73), calls=%async_computation.3 | async-start | bytes 2097152 | tf_op jit(solution)/shard_map/all_to_all | solution.py:73
  46.1 11.8 %all-to-all-done.3 = bf16[128,4,1024]{2,0,1:T(8,128)(2,1)S(1)} async-done(((bf16[128,4,1024]{2,0,1:T(8,128)(2,1)}), bf16[128,4,1024]{2,0,1:T(8,128)(2,1)S(1)}, u32[]{:S(2)}, u32[]{:S(2)}) %all-to-all-start.3) | async-done | bytes 1048608 | tf_op jit(solution)/shard_map/all_to_all | solution.py:73
  58.6 2.6 %fusion.3 = (f32[2,4,512]{2,1,0:T(4,128)S(1)}, f32[2,512,512,4]{2,1,3,0:T(8,128)S(1)}) fusion(pred[512,512]{0,1:T(8,128)(4,1)S(1)} %fusion.8, bf16[512,2,4,128]{3,2,1,0:T(4,128)(2,1)S(1)} %reshape.174, bf16[512,2,128,1]{2,1,0,3:T(2,128)(2,1)} %bitcast.92), kind=kOutput, calls=%fused_computation.7 | convolution fusion | flops 543158272 | bytes 9977856 | tf_op jit(solution)/shard_map/bkgd,skd->kgbs/dot_general | solution.py:30
  61.2 1.8 %exponential_reduce_fusion = f32[2,4,512]{2,1,0:T(4,128)S(1)} fusion(f32[2,512,512,4]{2,1,3,0:T(8,128)S(1)} %get-tuple-element.10, f32[2,4,512]{2,1,0:T(4,128)S(1)} %get-tuple-element.9, pred[512,512]{0,1:T(8,128)(4,1)S(1)} %fusion.8), kind=kLoop, calls=%fused_computation.5 | loop fusion | flops 8384512 | bytes 8683520 | tf_op jit(solution)/shard_map/reduce_sum | solution.py:110
  63.0 2.1 %convolution_bitcast_fusion = bf16[512,2,128]{2,0,1:T(8,128)(2,1)S(1)} fusion(bf16[512,2,4,128]{3,2,1,0:T(4,128)(2,1)S(1)} %reshape.176, f32[2,512,512,4]{2,1,3,0:T(8,128)S(1)} %get-tuple-element.10, f32[2,4,512]{2,1,0:T(4,128)S(1)} %bitcast.100, pred[512,512]{0,1:T(8,128)(4,1)S(1)} %fusion.8), kind=kOutput, calls=%fused_computation.13 | convolution fusion | flops 545259520 | bytes 9977856 | tf_op jit(solution)/shard_map/kgbs,bkgd->skd/dot_general | solution.py:41
  65.4 0.9 all_to_all.100
  66.3 3.6 %all-to-all-start.6 = ((bf16[4,128,256]{2,1,0:T(8,128)(2,1)}), bf16[4,128,256]{2,1,0:T(8,128)(2,1)S(1)}, u32[]{:S(2)}, u32[]{:S(2)}) async-start(bf16[4,128,256]{2,1,0:T(8,128)(2,1)} %all_to_all.100), calls=%async_computation.6 | async-start | bytes 524288 | tf_op jit(solution)/shard_map/all_to_all | solution.py:150
  69.9 5.9 %fusion.4 = f32[2,4,512,128]{3,2,1,0:T(8,128)S(1)} fusion(bf16[512,2,128,1]{2,1,0,3:T(2,128)(2,1)S(1)} %bitcast.96, f32[2,512,512,4]{2,1,3,0:T(8,128)} %copy-done, f32[2,4,512]{2,1,0:T(4,128)S(1)} %bitcast.101, pred[512,512]{0,1:T(8,128)(4,1)S(1)} %fusion.8), kind=kOutput, calls=%fused_computation.11 | convolution fusion | flops 546308096 | bytes 11026432 | tf_op jit(solution)/shard_map/kgbs,skd->bkgd/dot_general | solution.py:37
  75.8 2.1 %multiply_reduce_fusion = f32[2,4,512]{1,0,2:T(2,128)S(1)} fusion(f32[2,4,512,128]{3,2,1,0:T(8,128)S(1)} %fusion.4, bf16[512,2,4,128]{3,2,1,0:T(4,128)(2,1)S(1)} %reshape.176), kind=kLoop, calls=%fused_computation.8 | loop fusion | flops 1568768 | bytes 3162112
  78.1 5.1 %fusion.1 = bf16[2,4,512,512]{2,3,1,0:T(8,128)(2,1)S(1)} fusion(f32[2,512,512,4]{2,1,3,0:T(8,128)} %copy-done, f32[2,4,512]{2,1,0:T(4,128)S(1)} %copy.80, f32[2,4,512]{2,1,0:T(4,128)S(1)} %bitcast.102, pred[512,512]{0,1:T(8,128)(4,1)S(1)} %fusion.8, bf16[512,2,4,128]{3,2,1,0:T(4,128)(2,1)S(1)} %reshape.176, bf16[512,2,128,1]{2,1,0,3:T(2,128)(2,1)S(1)} %bitcast.97), kind=kOutput, calls=%fused_computation.2 | convolution fusion | flops 549453824 | bytes 14188544 | tf_op jit(solution)/shard_map/bkgd,skd->kgbs/dot_general | solution.py:44
  83.2 1.9 %copy-done.1 = bf16[2,4,512,512]{2,3,1,0:T(8,128)(2,1)} copy-done((bf16[2,4,512,512]{2,3,1,0:T(8,128)(2,1)}, bf16[2,4,512,512]{2,3,1,0:T(8,128)(2,1)S(1)}, u32[]{:S(2)}) %copy-start.1) | copy-done | bytes 4194328
  85.2 1.2 %fusion.7 = bf16[512,2,128]{2,0,1:T(8,128)(2,1)S(1)} fusion(bf16[2,4,512,512]{2,3,1,0:T(8,128)(2,1)S(1)} %fusion.1, bf16[512,2,4,128]{3,2,1,0:T(4,128)(2,1)S(1)} %reshape.174), kind=kOutput, calls=%fused_computation.16 | convolution fusion | flops 537133056 | bytes 5505024 | tf_op jit(solution)/shard_map/kgbs,bkgd->skd/dot_general | solution.py:52
  86.7 0.9 all_to_all.98
  87.6 3.4 %all-to-all-start.5 = ((bf16[4,128,256]{2,1,0:T(8,128)(2,1)}), bf16[4,128,256]{2,1,0:T(8,128)(2,1)S(1)}, u32[]{:S(2)}, u32[]{:S(2)}) async-start(bf16[4,128,256]{2,1,0:T(8,128)(2,1)} %all_to_all.98), calls=%async_computation.5 | async-start | bytes 524288 | tf_op jit(solution)/shard_map/all_to_all | solution.py:149
  91.0 3.9 %fusion.5 = bf16[512,2,4,128]{3,0,2,1:T(8,128)(2,1)S(1)} fusion(bf16[2,4,512,512]{2,3,1,0:T(8,128)(2,1)} %copy-done.1, bf16[512,2,128,1]{2,1,0,3:T(2,128)(2,1)S(1)} %bitcast.93), kind=kOutput, calls=%fused_computation.12 | convolution fusion | flops 537919488 | bytes 5505024 | tf_op jit(solution)/shard_map/kgbs,skd->bkgd/dot_general | solution.py:48
  94.9 0.8 copy.59
  95.7 1.5 %all_to_all.94 = bf16[4,128,1024]{2,1,0:T(8,128)(2,1)} reshape(bf16[512,2,4,128]{3,2,1,0:T(4,128)(2,1)S(1)} %copy.59) | data formatting | bytes 2097152 | tf_op jit(solution)/shard_map/all_to_all | solution.py:147
  97.3 3.5 %all-to-all-start.4 = ((bf16[4,128,1024]{2,1,0:T(8,128)(2,1)}), bf16[4,128,1024]{2,1,0:T(8,128)(2,1)S(1)}, u32[]{:S(2)}, u32[]{:S(2)}) async-start(bf16[4,128,1024]{2,1,0:T(8,128)(2,1)} %all_to_all.94), calls=%async_computation.4 | async-start | bytes 2097152 | tf_op jit(solution)/shard_map/all_to_all | solution.py:147
  101.0 0.9 copy.69
  102.0 0.9 copy.68
  102.9 12.3 %all-to-all-done.4 = bf16[4,128,1024]{2,1,0:T(8,128)(2,1)S(1)} async-done(((bf16[4,128,1024]{2,1,0:T(8,128)(2,1)}), bf16[4,128,1024]{2,1,0:T(8,128)(2,1)S(1)}, u32[]{:S(2)}, u32[]{:S(2)}) %all-to-all-start.4) | async-done | bytes 1048608 | tf_op jit(solution)/shard_map/all_to_all | solution.py:147
  115.9 1.3 %copy.67 = bf16[128,4096]{1,0:T(8,128)(2,1)} copy(bf16[128,4096]{0,1:T(8,128)(2,1)S(1)} %bitcast.83) | data formatting | bytes 2097152
  (28 shorter events, 5.3 us)
Async XLA Ops:
  0.6 27.2 %copy-start.4 = (s32[8]{0:T(128)S(1)}, s32[8]{0:T(128)}, u32[]{:S(2)}) copy-start(s32[8]{0:T(128)} %param.9) | copy-start | bytes 100
  2.3 10.3 %all-to-all-start = ((bf16[128,4,256]{2,0,1:T(8,128)(2,1)}), bf16[128,4,256]{2,0,1:T(8,128)(2,1)S(1)}, u32[]{:S(2)}, u32[]{:S(2)}) async-start(bf16[128,4,256]{2,0,1:T(8,128)(2,1)} %bitcast.76), calls=%async_computation | async-start | bytes 524288 | tf_op jit(solution)/shard_map/all_to_all | solution.py:68
  12.6 9.4 %all-to-all-start.2 = ((bf16[128,4,256]{2,0,1:T(8,128)(2,1)}), bf16[128,4,256]{2,0,1:T(8,128)(2,1)S(1)}, u32[]{:S(2)}, u32[]{:S(2)}) async-start(bf16[128,4,256]{2,0,1:T(8,128)(2,1)} %bitcast.75), calls=%async_computation.2 | async-start | bytes 524288 | tf_op jit(solution)/shard_map/all_to_all | solution.py:69
  22.0 17.9 %all-to-all-start.1 = ((bf16[128,4,1024]{2,0,1:T(8,128)(2,1)}), bf16[128,4,1024]{2,0,1:T(8,128)(2,1)S(1)}, u32[]{:S(2)}, u32[]{:S(2)}) async-start(bf16[128,4,1024]{2,0,1:T(8,128)(2,1)} %bitcast.74), calls=%async_computation.1 | async-start | bytes 2097152 | tf_op jit(solution)/shard_map/all_to_all | solution.py:72
  39.9 17.9 %all-to-all-start.3 = ((bf16[128,4,1024]{2,0,1:T(8,128)(2,1)}), bf16[128,4,1024]{2,0,1:T(8,128)(2,1)S(1)}, u32[]{:S(2)}, u32[]{:S(2)}) async-start(bf16[128,4,1024]{2,0,1:T(8,128)(2,1)} %bitcast.73), calls=%async_computation.3 | async-start | bytes 2097152 | tf_op jit(solution)/shard_map/all_to_all | solution.py:73
  61.2 3.9 %copy-start = (f32[2,512,512,4]{2,1,3,0:T(8,128)}, f32[2,512,512,4]{2,1,3,0:T(8,128)S(1)}, u32[]{:S(2)}) copy-start(f32[2,512,512,4]{2,1,3,0:T(8,128)S(1)} %get-tuple-element.10) | copy-start | bytes 25165828
  63.0 6.9 %copy-start.3 = (bf16[512,2,128]{2,1,0:T(2,128)(2,1)S(1)}, bf16[512,2,128]{2,1,0:T(2,128)(2,1)}, u32[]{:S(2)}) copy-start(bf16[512,2,128]{2,1,0:T(2,128)(2,1)} %reshape.175) | copy-start | bytes 786436
  66.3 21.3 %all-to-all-start.6 = ((bf16[4,128,256]{2,1,0:T(8,128)(2,1)}), bf16[4,128,256]{2,1,0:T(8,128)(2,1)S(1)}, u32[]{:S(2)}, u32[]{:S(2)}) async-start(bf16[4,128,256]{2,1,0:T(8,128)(2,1)} %all_to_all.100), calls=%async_computation.6 | async-start | bytes 524288 | tf_op jit(solution)/shard_map/all_to_all | solution.py:150
  78.1 12.9 %copy-start.2 = (bf16[512,2,128]{2,1,0:T(2,128)(2,1)S(1)}, bf16[512,2,128]{2,1,0:T(2,128)(2,1)}, u32[]{:S(2)}) copy-start(bf16[512,2,128]{2,1,0:T(2,128)(2,1)} %reshape.173) | copy-start | bytes 786436
  83.2 1.9 %copy-start.1 = (bf16[2,4,512,512]{2,3,1,0:T(8,128)(2,1)}, bf16[2,4,512,512]{2,3,1,0:T(8,128)(2,1)S(1)}, u32[]{:S(2)}) copy-start(bf16[2,4,512,512]{2,3,1,0:T(8,128)(2,1)S(1)} %fusion.1) | copy-start | bytes 12582916
  87.6 9.7 %all-to-all-start.5 = ((bf16[4,128,256]{2,1,0:T(8,128)(2,1)}), bf16[4,128,256]{2,1,0:T(8,128)(2,1)S(1)}, u32[]{:S(2)}, u32[]{:S(2)}) async-start(bf16[4,128,256]{2,1,0:T(8,128)(2,1)} %all_to_all.98), calls=%async_computation.5 | async-start | bytes 524288 | tf_op jit(solution)/shard_map/all_to_all | solution.py:149
  97.3 17.9 %all-to-all-start.4 = ((bf16[4,128,1024]{2,1,0:T(8,128)(2,1)}), bf16[4,128,1024]{2,1,0:T(8,128)(2,1)S(1)}, u32[]{:S(2)}, u32[]{:S(2)}) async-start(bf16[4,128,1024]{2,1,0:T(8,128)(2,1)} %all_to_all.94), calls=%async_computation.4 | async-start | bytes 2097152 | tf_op jit(solution)/shard_map/all_to_all | solution.py:147
where the time goes:
time: 118 us; the launch traced here: 117 us
  waiting for transfers between devices  44 us (37%)
  starting transfers between devices  25.2 us (21%)
  local copies, waits for them, and re-layouts  21.7 us (18%)
  matrix products  21 us (18%)
  other arithmetic  4.36 us (4%)
    all_to_all x1, waiting for transfers between devices, on_device(): lax.all_to_all(query_local, 'sp', split_axis=0, concat_axis=1, tiled=True)  12.3 us
    all_to_all x1, waiting for transfers between devices, on_device(): lax.all_to_all(query_rows, 'sp', split_axis=1, concat_axis=0, tiled=True)  11.9 us
    all_to_all x1, waiting for transfers between devices, on_device(): lax.all_to_all(out_grad, 'sp', split_axis=1, concat_axis=0, tiled=True)  11.8 us
    dot_general x1, matrix products, weighted_values(): jnp.einsum('kgbs,skd->bkgd', probs_b, value_block, preferred_element_type...  5.91 us
    dot_general x1, matrix products, backward_block(): jnp.einsum('bkgd,skd->kgbs', grad_block, value_block, preferred_element_t...  5.15 us
    unnamed x13, local copies, waits for them, and re-layouts  4.96 us
    all_to_all x1, waiting for transfers between devices, on_device(): lax.all_to_all(widen(key_rows, copies), 'sp', split_axis=1, concat_axis=0...  4.34 us
    all_to_all x1, starting transfers between devices, on_device(): lax.all_to_all(widen(key_rows, copies), 'sp', split_axis=1, concat_axis=0...  4.26 us
  transfers between devices with their start and end apart: 7, of which 5 were waited for; matrix products, arithmetic and copies ran while one was open for 26% of the time, Pallas kernels for 0%

commit v1 on v0

--- a/solution.py
+++ b/solution.py
@@ -10,6 +10,13 @@
 QH = 32
 KVH = 8
 MASKED = -1e30
+
+
+def stacked_exchange(x, mesh_axis, split, join):
+    size = lax.axis_size(mesh_axis)
+    shards = jnp.stack(jnp.split(x, size, axis=split), axis=0)
+    shards = lax.all_to_all(shards, mesh_axis, split_axis=0, concat_axis=0)
+    return jnp.concatenate(shards, axis=join)
 
 
 def widen(rows, copies):
@@ -70,7 +77,7 @@
     )
     queries_local, grads_local = (
         lax.all_to_all(query_rows, "sp", split_axis=1, concat_axis=0, tiled=True),
-        lax.all_to_all(out_grad, "sp", split_axis=1, concat_axis=0, tiled=True),
+        stacked_exchange(out_grad, "sp", 1, 0),
     )
     key_heads = KVH * copies // devices
     per_group = QH // devices // key_heads

time: 118 us -> 114 us (0.966)
  local copies, waits for them, and re-layouts: 21.7 us -> 19.8 us
  waiting for transfers between devices: 44 us -> 42.2 us
  matrix products: 21 us -> 19.7 us
    all_to_all x1, waiting for transfers between devices: 11.9 us -> 7.36 us  [on_device(): lax.all_to_all(query_rows, 'sp', split_axis=1, concat_axis=0, tiled=True)]
    another operation x0 -> x3, local copies, waits for them, and re-layouts: none -> 2.97 us  [the longest x2 1.71 us: on_device(): grads = grads_local.reshape(length, key_heads, per_group, HD)]
    dot_general x1, matrix products: 5.91 us -> 3.15 us  [weighted_values(): jnp.einsum('kgbs,skd->bkgd', probs_b, value_block, preferred_element_type...]
    all_to_all x1 -> x0, local copies, waits for them, and re-layouts: 2.29 us -> none  [on_device(): lax.all_to_all(out_grad, 'sp', split_axis=1, concat_axis=0, tiled=True)]
    dot_general x1, matrix products: 1.24 us -> 3.43 us  [backward_block(): jnp.einsum('kgbs,bkgd->skd', score_grad, query_block, preferred_element_t...]
    unnamed x13 -> x15, local copies, waits for them, and re-layouts: 4.96 us -> 3.04 us
    all_to_all x1, waiting for transfers between devices: 11.8 us -> 13.1 us  [stacked_exchange(): shards = lax.all_to_all(shards, mesh_axis, split_axis=0, concat_axis=0)]
    all_to_all x1, local copies, waits for them, and re-layouts: 2.29 us -> 1.06 us  [on_device(): lax.all_to_all(query_rows, 'sp', split_axis=1, concat_axis=0, tiled=True)]
  transfers between devices with their start and end apart: 7 -> 7, of which waited for: 5 -> 6; matrix products, arithmetic and copies ran while one was open for 26% -> 20% of each run, Pallas kernels for 0% -> 0%
where the time goes in v1:
time: 114 us; the launch traced here: 113 us
  waiting for transfers between devices  42.2 us (37%)
  starting transfers between devices  25.9 us (23%)
  local copies, waits for them, and re-layouts  19.8 us (17%)
  matrix products  19.7 us (17%)
  other arithmetic  5.01 us (4%)
    all_to_all x1, waiting for transfers between devices, stacked_exchange(): shards = lax.all_to_all(shards, mesh_axis, split_axis=0, concat_axis=0)  13.1 us
    all_to_all x1, waiting for transfers between devices, on_device(): lax.all_to_all(query_local, 'sp', split_axis=0, concat_axis=1, tiled=True)  12.5 us
    all_to_all x1, waiting for transfers between devices, on_device(): lax.all_to_all(query_rows, 'sp', split_axis=1, concat_axis=0, tiled=True)  7.36 us
    all_to_all x1, waiting for transfers between devices, on_device(): lax.all_to_all(widen(key_rows, copies), 'sp', split_axis=1, concat_axis=0...  4.34 us
    all_to_all x1, starting transfers between devices, on_device(): lax.all_to_all(widen(key_rows, copies), 'sp', split_axis=1, concat_axis=0...  4.26 us
    dot_general x1, matrix products, backward_block(): jnp.einsum('bkgd,skd->kgbs', grad_block, value_block, preferred_element_t...  4.1 us
    all_to_all x1, starting transfers between devices, on_device(): lax.all_to_all(widen(value_rows, copies), 'sp', split_axis=1, concat_axis...  4.04 us
    dot_general x1, matrix products, backward_block(): jnp.einsum('kgbs,skd->bkgd', score_grad, key_block, preferred_element_typ...  3.93 us
  transfers between devices with their start and end apart: 7, of which 6 were waited for; matrix products, arithmetic and copies ran while one was open for 20% of the time, Pallas kernels for 0%

profile of v1, /device:TPU:0, one launch (start us, length us, event | category | flops | bytes accessed | tf_op | source)
XLA Modules:
  0.0 113.4 jit_solution(10422318579550234543)
XLA Ops:
  0.7 1.8 %copy.146 = bf16[16,4,8,256]{3,2,0,1:T(8,128)(2,1)} copy(bf16[16,4,8,256]{3,2,1,0:T(8,128)(2,1)} %bitcast.96) | data formatting | bytes 524288 | tf_op jit(solution)/shard_map/all_to_all | solution.py:75
  2.4 4.3 %all-to-all-start = ((bf16[128,4,256]{2,0,1:T(8,128)(2,1)}), bf16[128,4,256]{2,0,1:T(8,128)(2,1)S(1)}, u32[]{:S(2)}, u32[]{:S(2)}) async-start(bf16[128,4,256]{2,0,1:T(8,128)(2,1)} %bitcast.82), calls=%async_computation | async-start | bytes 524288 | tf_op jit(solution)/shard_map/all_to_all | solution.py:75
  6.7 1.7 %copy.145 = bf16[16,4,8,256]{3,2,0,1:T(8,128)(2,1)} copy(bf16[16,4,8,256]{3,2,1,0:T(8,128)(2,1)} %bitcast.97) | data formatting | bytes 524288 | tf_op jit(solution)/shard_map/all_to_all | solution.py:76
  8.3 4.3 %all-to-all-done = bf16[128,4,256]{2,0,1:T(8,128)(2,1)S(1)} async-done(((bf16[128,4,256]{2,0,1:T(8,128)(2,1)}), bf16[128,4,256]{2,0,1:T(8,128)(2,1)S(1)}, u32[]{:S(2)}, u32[]{:S(2)}) %all-to-all-start) | async-done | bytes 262176 | tf_op jit(solution)/shard_map/all_to_all | solution.py:75
  12.7 4.0 %all-to-all-start.3 = ((bf16[128,4,256]{2,0,1:T(8,128)(2,1)}), bf16[128,4,256]{2,0,1:T(8,128)(2,1)}, u32[]{:S(2)}, u32[]{:S(2)}) async-start(bf16[128,4,256]{2,0,1:T(8,128)(2,1)} %bitcast.81), calls=%async_computation.3 | async-start | bytes 524288 | tf_op jit(solution)/shard_map/all_to_all | solution.py:76
  16.7 1.3 %slice_bitcast_fusion.3 = (bf16[1,128,1024]{2,1,0:T(8,128)(2,1)S(1)}, bf16[1,128,1024]{2,1,0:T(8,128)(2,1)S(1)}, bf16[1,128,1024]{2,1,0:T(8,128)(2,1)S(1)}, bf16[1,128,1024]{2,1,0:T(8,128)(2,1)S(1)}) fusion(bf16[128,4096]{1,0:T(8,128)(2,1)} %param.8), kind=kLoop, calls=%fused_computation.30 | loop fusion | bytes 2097152 | tf_op jit(solution)/shard_map/stack | solution.py:17
  18.0 1.1 pad_maximum_fusion
  19.1 3.7 %all-to-all-done.3 = bf16[128,4,256]{2,0,1:T(8,128)(2,1)} async-done(((bf16[128,4,256]{2,0,1:T(8,128)(2,1)}), bf16[128,4,256]{2,0,1:T(8,128)(2,1)}, u32[]{:S(2)}, u32[]{:S(2)}) %all-to-all-start.3) | async-done | bytes 262176 | tf_op jit(solution)/shard_map/all_to_all | solution.py:76
  22.8 3.5 %all-to-all-start.2 = ((bf16[4,128,1024]{2,1,0:T(8,128)(2,1)}), bf16[4,128,1024]{2,1,0:T(8,128)(2,1)S(1)}, u32[]{:S(2)}, u32[]{:S(2)}) async-start(bf16[4,128,1024]{2,1,0:T(8,128)(2,1)} %pad_maximum_fusion), calls=%async_computation.2 | async-start | bytes 2097152 | tf_op jit(solution)/shard_map/all_to_all | solution.py:18
  26.3 1.1 copy.144
  27.7 13.1 %all-to-all-done.2 = bf16[4,128,1024]{2,1,0:T(8,128)(2,1)S(1)} async-done(((bf16[4,128,1024]{2,1,0:T(8,128)(2,1)}), bf16[4,128,1024]{2,1,0:T(8,128)(2,1)S(1)}, u32[]{:S(2)}, u32[]{:S(2)}) %all-to-all-start.2) | async-done | bytes 1048608 | tf_op jit(solution)/shard_map/all_to_all | solution.py:18
  40.7 3.5 %all-to-all-start.1 = ((bf16[128,4,1024]{2,0,1:T(8,128)(2,1)}), bf16[128,4,1024]{2,0,1:T(8,128)(2,1)S(1)}, u32[]{:S(2)}, u32[]{:S(2)}) async-start(bf16[128,4,1024]{2,0,1:T(8,128)(2,1)} %bitcast.80), calls=%async_computation.1 | async-start | bytes 2097152 | tf_op jit(solution)/shard_map/all_to_all | solution.py:79
  44.5 1.7 %reshape.166 = bf16[512,2,128]{2,1,0:T(2,128)(2,1)} reshape(bf16[4,128,256]{2,1,0:T(8,128)(2,1)} %bitcast.90) | data formatting | bytes 524288 | tf_op jit(solution)/shard_map/reshape | solution.py:86
  46.2 1.7 %reshape.168 = bf16[512,2,128]{2,1,0:T(2,128)(2,1)} reshape(bf16[4,128,256]{2,1,0:T(8,128)(2,1)} %bitcast.12) | data formatting | bytes 524288 | tf_op jit(solution)/shard_map/reshape | solution.py:87
  48.7 1.0 copy.91
  49.7 1.6 %bitcast_convert_fusion = f32[2,4,512,128]{3,1,0,2:T(4,128)} fusion(bf16[512,2,4,128]{3,2,1,0:T(4,128)(2,1)S(1)} %reshape_reshape.3), kind=kLoop, calls=%fused_computation.18 | loop fusion | flops 524288 | bytes 3145728
  51.3 7.4 %all-to-all-done.1 = bf16[128,4,1024]{2,0,1:T(8,128)(2,1)S(1)} async-done(((bf16[128,4,1024]{2,0,1:T(8,128)(2,1)}), bf16[128,4,1024]{2,0,1:T(8,128)(2,1)S(1)}, u32[]{:S(2)}, u32[]{:S(2)}) %all-to-all-start.1) | async-done | bytes 1048608 | tf_op jit(solution)/shard_map/all_to_all | solution.py:79
  59.4 2.6 %fusion.3 = (f32[2,4,512]{2,1,0:T(4,128)S(1)}, f32[2,512,512,4]{2,1,3,0:T(8,128)S(1)}) fusion(pred[512,512]{0,1:T(8,128)(4,1)S(1)} %fusion.7, bf16[512,2,4,128]{3,2,1,0:T(4,128)(2,1)S(1)} %reshape.167, bf16[512,2,128,1]{2,1,0,3:T(2,128)(2,1)} %bitcast.94), kind=kOutput, calls=%fused_computation.7 | convolution fusion | flops 543158272 | bytes 9977856 | tf_op jit(solution)/shard_map/bkgd,skd->kgbs/dot_general | solution.py:37
  62.0 1.8 %exponential_reduce_fusion = f32[2,4,512]{2,1,0:T(4,128)S(1)} fusion(f32[2,512,512,4]{2,1,3,0:T(8,128)S(1)} %get-tuple-element.17, f32[2,4,512]{2,1,0:T(4,128)S(1)} %get-tuple-element.16, pred[512,512]{0,1:T(8,128)(4,1)S(1)} %fusion.7), kind=kLoop, calls=%fused_computation.5 | loop fusion | flops 8384512 | bytes 8683520 | tf_op jit(solution)/shard_map/reduce_sum | solution.py:117
  63.8 2.5 %convolution_bitcast_fusion = bf16[512,2,128]{0,2,1:T(8,128)(2,1)S(1)} fusion(bf16[512,2,4,128]{0,3,2,1:T(8,128)(2,1)S(1)} %copy.91, f32[2,512,512,4]{2,1,3,0:T(8,128)S(1)} %get-tuple-element.17, f32[2,4,512]{2,1,0:T(4,128)S(1)} %bitcast.102, pred[512,512]{0,1:T(8,128)(4,1)S(1)} %fusion.7), kind=kOutput, calls=%fused_computation.12 | convolution fusion | flops 545259520 | bytes 9977856 | tf_op jit(solution)/shard_map/kgbs,bkgd->skd/dot_general | solution.py:48
  66.3 3.1 %multiply_reduce_fusion = f32[2,4,512]{2,1,0:T(4,128)S(1)} fusion(f32[2,4,512,128]{3,1,0,2:T(4,128)S(1)} %copy-done, bf16[512,2,128,1]{2,1,0,3:T(2,128)(2,1)S(1)} %bitcast.98, f32[2,512,512,4]{2,1,3,0:T(8,128)S(1)} %get-tuple-element.17, f32[2,4,512]{2,1,0:T(4,128)S(1)} %bitcast.103, pred[512,512]{0,1:T(8,128)(4,1)S(1)} %fusion.7), kind=kOutput, calls=%fused_computation.8 | convolution fusion | flops 547352576 | bytes 11042816 | tf_op jit(solution)/shard_map/kgbs,skd->bkgd/dot_general | solution.py:44
  69.5 4.1 %fusion.1 = bf16[2,4,512,512]{2,3,1,0:T(8,128)(2,1)} fusion(f32[2,512,512,4]{2,1,3,0:T(8,128)S(1)} %get-tuple-element.17, f32[2,4,512]{2,1,0:T(4,128)S(1)} %multiply_reduce_fusion, f32[2,4,512]{2,1,0:T(4,128)S(1)} %bitcast.104, pred[512,512]{0,1:T(8,128)(4,1)S(1)} %fusion.7, bf16[512,2,4,128]{0,3,2,1:T(8,128)(2,1)S(1)} %copy.91, ...), kind=kOutput, calls=%fused_computation.2 | convolution fusion | flops 549453824 | bytes 14188544 | tf_op jit(solution)/shard_map/bkgd,skd->kgbs/dot_general | solution.py:51
  74.4 3.6 %all-to-all-start.6 = ((bf16[4,128,256]{1,2,0:T(8,128)(2,1)}), bf16[4,128,256]{1,2,0:T(8,128)(2,1)S(1)}, u32[]{:S(2)}, u32[]{:S(2)}) async-start(bf16[4,128,256]{1,2,0:T(8,128)(2,1)} %copy.93), calls=%async_computation.6 | async-start | bytes 524288 | tf_op jit(solution)/shard_map/all_to_all | solution.py:157
  78.0 3.4 %fusion.6 = bf16[512,2,128]{2,0,1:T(8,128)(2,1)S(1)} fusion(bf16[2,4,512,512]{2,3,1,0:T(8,128)(2,1)} %fusion.1, bf16[512,2,4,128]{3,2,1,0:T(4,128)(2,1)S(1)} %reshape.167), kind=kOutput, calls=%fused_computation.15 | convolution fusion | flops 537133056 | bytes 5505024 | tf_op jit(solution)/shard_map/kgbs,bkgd->skd/dot_general | solution.py:59
  81.7 0.9 all_to_all.87
  82.6 1.2 %all-to-all-done.6 = bf16[4,128,256]{1,2,0:T(8,128)(2,1)S(1)} async-done(((bf16[4,128,256]{1,2,0:T(8,128)(2,1)}), bf16[4,128,256]{1,2,0:T(8,128)(2,1)S(1)}, u32[]{:S(2)}, u32[]{:S(2)}) %all-to-all-start.6) | async-done | bytes 262176 | tf_op jit(solution)/shard_map/all_to_all | solution.py:157
  83.8 3.4 %all-to-all-start.5 = ((bf16[4,128,256]{2,1,0:T(8,128)(2,1)}), bf16[4,128,256]{2,1,0:T(8,128)(2,1)S(1)}, u32[]{:S(2)}, u32[]{:S(2)}) async-start(bf16[4,128,256]{2,1,0:T(8,128)(2,1)} %all_to_all.87), calls=%async_computation.5 | async-start | bytes 524288 | tf_op jit(solution)/shard_map/all_to_all | solution.py:156
  87.2 3.9 %fusion.4 = bf16[512,2,4,128]{3,0,2,1:T(8,128)(2,1)S(1)} fusion(bf16[2,4,512,512]{2,3,1,0:T(8,128)(2,1)} %fusion.1, bf16[512,2,128,1]{2,1,0,3:T(2,128)(2,1)S(1)} %bitcast.95), kind=kOutput, calls=%fused_computation.11 | convolution fusion | flops 537919488 | bytes 5505024 | tf_op jit(solution)/shard_map/kgbs,skd->bkgd/dot_general | solution.py:55
  92.0 1.5 %all_to_all.83 = bf16[4,128,1024]{2,1,0:T(8,128)(2,1)} reshape(bf16[512,2,4,128]{3,2,1,0:T(4,128)(2,1)S(1)} %copy.86) | data formatting | bytes 2097152 | tf_op jit(solution)/shard_map/all_to_all | solution.py:154
  93.5 3.5 %all-to-all-start.4 = ((bf16[4,128,1024]{2,1,0:T(8,128)(2,1)}), bf16[4,128,1024]{2,1,0:T(8,128)(2,1)S(1)}, u32[]{:S(2)}, u32[]{:S(2)}) async-start(bf16[4,128,1024]{2,1,0:T(8,128)(2,1)} %all_to_all.83), calls=%async_computation.4 | async-start | bytes 2097152 | tf_op jit(solution)/shard_map/all_to_all | solution.py:154
  98.9 12.5 %all-to-all-done.4 = bf16[4,128,1024]{2,1,0:T(8,128)(2,1)S(1)} async-done(((bf16[4,128,1024]{2,1,0:T(8,128)(2,1)}), bf16[4,128,1024]{2,1,0:T(8,128)(2,1)S(1)}, u32[]{:S(2)}, u32[]{:S(2)}) %all-to-all-start.4) | async-done | bytes 1048608 | tf_op jit(solution)/shard_map/all_to_all | solution.py:154
  112.1 1.3 %copy.94 = bf16[128,4096]{1,0:T(8,128)(2,1)} copy(bf16[128,4096]{0,1:T(8,128)(2,1)S(1)} %bitcast.88) | data formatting | bytes 2097152
  (30 shorter events, 6.5 us)
Async XLA Ops:
  0.6 25.7 %copy-start.1 = (bf16[128,4096]{1,0:T(8,128)(2,1)S(1)}, bf16[128,4096]{1,0:T(8,128)(2,1)}, u32[]{:S(2)}) copy-start(bf16[128,4096]{1,0:T(8,128)(2,1)} %param.5) | copy-start | bytes 3145732
  0.6 26.8 %copy-start.5 = (s32[8]{0:T(128)S(1)}, s32[8]{0:T(128)}, u32[]{:S(2)}) copy-start(s32[8]{0:T(128)} %param.9) | copy-start | bytes 100
  2.4 10.3 %all-to-all-start = ((bf16[128,4,256]{2,0,1:T(8,128)(2,1)}), bf16[128,4,256]{2,0,1:T(8,128)(2,1)S(1)}, u32[]{:S(2)}, u32[]{:S(2)}) async-start(bf16[128,4,256]{2,0,1:T(8,128)(2,1)} %bitcast.82), calls=%async_computation | async-start | bytes 524288 | tf_op jit(solution)/shard_map/all_to_all | solution.py:75
  12.7 10.1 %copy-start.2 = (bf16[128,4,256]{2,0,1:T(8,128)(2,1)}, bf16[128,4,256]{2,0,1:T(8,128)(2,1)S(1)}, u32[]{:S(2)}) copy-start(bf16[128,4,256]{2,0,1:T(8,128)(2,1)S(1)} %all-to-all-done) | copy-start | bytes 786436
  12.7 10.1 %all-to-all-start.3 = ((bf16[128,4,256]{2,0,1:T(8,128)(2,1)}), bf16[128,4,256]{2,0,1:T(8,128)(2,1)}, u32[]{:S(2)}, u32[]{:S(2)}) async-start(bf16[128,4,256]{2,0,1:T(8,128)(2,1)} %bitcast.81), calls=%async_computation.3 | async-start | bytes 524288 | tf_op jit(solution)/shard_map/all_to_all | solution.py:76
  22.8 17.9 %all-to-all-start.2 = ((bf16[4,128,1024]{2,1,0:T(8,128)(2,1)}), bf16[4,128,1024]{2,1,0:T(8,128)(2,1)S(1)}, u32[]{:S(2)}, u32[]{:S(2)}) async-start(bf16[4,128,1024]{2,1,0:T(8,128)(2,1)} %pad_maximum_fusion), calls=%async_computation.2 | async-start | bytes 2097152 | tf_op jit(solution)/shard_map/all_to_all | solution.py:18
  40.7 17.9 %all-to-all-start.1 = ((bf16[128,4,1024]{2,0,1:T(8,128)(2,1)}), bf16[128,4,1024]{2,0,1:T(8,128)(2,1)S(1)}, u32[]{:S(2)}, u32[]{:S(2)}) async-start(bf16[128,4,1024]{2,0,1:T(8,128)(2,1)} %bitcast.80), calls=%async_computation.1 | async-start | bytes 2097152 | tf_op jit(solution)/shard_map/all_to_all | solution.py:79
  63.8 2.5 %copy-start = (f32[2,4,512,128]{3,1,0,2:T(4,128)S(1)}, f32[2,4,512,128]{3,1,0,2:T(4,128)}, u32[]{:S(2)}) copy-start(f32[2,4,512,128]{3,1,0,2:T(4,128)} %bitcast_convert_fusion) | copy-start | bytes 6291460
  63.8 2.5 %copy-start.4 = (bf16[512,2,128]{2,1,0:T(2,128)(2,1)S(1)}, bf16[512,2,128]{2,1,0:T(2,128)(2,1)}, u32[]{:S(2)}) copy-start(bf16[512,2,128]{2,1,0:T(2,128)(2,1)} %reshape.168) | copy-start | bytes 786436
  73.6 13.6 %copy-start.3 = (bf16[512,2,128]{2,1,0:T(2,128)(2,1)S(1)}, bf16[512,2,128]{2,1,0:T(2,128)(2,1)}, u32[]{:S(2)}) copy-start(bf16[512,2,128]{2,1,0:T(2,128)(2,1)} %reshape.166) | copy-start | bytes 786436
  74.4 9.4 %all-to-all-start.6 = ((bf16[4,128,256]{1,2,0:T(8,128)(2,1)}), bf16[4,128,256]{1,2,0:T(8,128)(2,1)S(1)}, u32[]{:S(2)}, u32[]{:S(2)}) async-start(bf16[4,128,256]{1,2,0:T(8,128)(2,1)} %copy.93), calls=%async_computation.6 | async-start | bytes 524288 | tf_op jit(solution)/shard_map/all_to_all | solution.py:157
  83.8 9.7 %all-to-all-start.5 = ((bf16[4,128,256]{2,1,0:T(8,128)(2,1)}), bf16[4,128,256]{2,1,0:T(8,128)(2,1)S(1)}, u32[]{:S(2)}, u32[]{:S(2)}) async-start(bf16[4,128,256]{2,1,0:T(8,128)(2,1)} %all_to_all.87), calls=%async_computation.5 | async-start | bytes 524288 | tf_op jit(solution)/shard_map/all_to_all | solution.py:156
  93.5 17.9 %all-to-all-start.4 = ((bf16[4,128,1024]{2,1,0:T(8,128)(2,1)}), bf16[4,128,1024]{2,1,0:T(8,128)(2,1)S(1)}, u32[]{:S(2)}, u32[]{:S(2)}) async-start(bf16[4,128,1024]{2,1,0:T(8,128)(2,1)} %all_to_all.83), calls=%async_computation.4 | async-start | bytes 2097152 | tf_op jit(solution)/shard_map/all_to_all | solution.py:154
